TPU v7x, 32 devices: a whole 2x2x4 slice. The times are simulated.
32 devices in a mesh: dp: 8 (over z, y), mp: 4 (over x, core).
Axes of the slice: x: 2, y: 2, z: 4, core: 2. Of those that a mesh axis runs over, the one named last changes fastest.
Arguments:
- streams: bfloat16 [2048, 4, 8192], P('dp', None, 'mp'), may hold values from -200 to 200
- branch_out: bfloat16 [2048, 8192], P('dp', 'mp'), may hold values from -6 to 6
- merge_weight: float32 [20, 4, 8192], P(None, None, ('mp', 'dp')), may hold values from -0.03125 to 0.03125
- next_weight: float32 [24, 4, 8192], P(None, None, ('mp', 'dp')), may hold values from -0.03125 to 0.03125
- blend_bias: float32 [44], replicated, may hold values from -3 to 3
- blend_scale: float32 [5], replicated, may hold values from 0.5 to 3
- norm_gain: float32 [8192], P('mp'), may hold values from 0.5 to 1.5
Outputs:
- streams_out: bfloat16 [2048, 4, 8192], P('dp', None, 'mp')
- branch_in: bfloat16 [2048, 8192], P('dp', 'mp')
- next_mix: float32 [2048, 20], P('dp')
All inputs are finite; a program needn't handle non-finite values.
Results may differ from a plain program's by a relative error of at most 0.001.
Values sent between devices are 32-bit elements; how exact they have to be, the bound alone decides.
No kernel may reach another device: no remote copies, remote signals or barrier semaphores. Data moves between devices by JAX's collectives and lax.ppermute only.
A program may use at most 64 MiB of HBM per device.

v0:
```python
import jax
import jax.numpy as jnp
from jax import lax
from jax.sharding import PartitionSpec as P

D = 8192
STREAMS = 4
BALANCE_ROUNDS = 6
epsilon = 1e-06


def balance_normalize(balanced_matrix):
    for balance_round in range(BALANCE_ROUNDS):
        balanced_matrix = balanced_matrix / jnp.sum(balanced_matrix, axis=2, keepdims=True)
        balanced_matrix = balanced_matrix / jnp.sum(balanced_matrix, axis=1, keepdims=True)
    return balanced_matrix


def settle(columns, finish):
    summed = lax.psum(columns, "mp")
    result = finish(summed)
    return result


def first_coef(raw_sums, squares, blend_bias, blend_scale):
    rms_root = jnp.sqrt(squares / (STREAMS * D) + epsilon)
    score_logits = raw_sums / rms_root[:, None]
    post_mix = 2.0 * jax.nn.sigmoid(blend_scale[0] * score_logits[:, :4] + blend_bias[:4])
    residual_blend = balance_normalize(
        jnp.exp(
            blend_scale[1] * score_logits[:, 4:20].reshape(-1, 4, 4)
            + blend_bias[4:20].reshape(4, 4)
        )
    )
    return (post_mix, residual_blend)


def second_coef(raw_sums, squares, blend_bias, blend_scale):
    rms_root = jnp.sqrt(squares / (STREAMS * D) + epsilon)
    score_logits = raw_sums / rms_root[:, None]
    pre_next = jax.nn.sigmoid(blend_scale[2] * score_logits[:, :4] + blend_bias[20:24])
    post_next = 2.0 * jax.nn.sigmoid(blend_scale[3] * score_logits[:, 4:8] + blend_bias[24:28])
    residual_following = balance_normalize(
        jnp.exp(
            blend_scale[4] * score_logits[:, 8:24].reshape(-1, 4, 4)
            + blend_bias[28:44].reshape(4, 4)
        )
    )
    return (pre_next, post_next, residual_following)


def mix_streams(residual_blend, post_mix, streams, branch_out):
    branch_wide = branch_out.astype(jnp.float32)
    outputs = []
    for target in range(STREAMS):
        total = post_mix[:, target, None] * branch_wide
        for source in range(STREAMS):
            total = total + residual_blend[:, target, source, None] * streams[:, source, :].astype(
                jnp.float32
            )
        outputs.append(total)
    return jnp.stack(outputs, axis=1)


def unite(pre_next, mixed):
    total = pre_next[:, 0, None] * mixed[:, 0, :]
    for source in range(1, STREAMS):
        total = total + pre_next[:, source, None] * mixed[:, source, :]
    return total


def local(streams, branch_out, merge_weight, next_weight, blend_bias, blend_scale, norm_gain):
    merge_rows, next_rows = (
        lax.all_gather(merge_weight, "dp", axis=2, tiled=True),
        lax.all_gather(next_weight, "dp", axis=2, tiled=True),
    )
    highest = lax.Precision.HIGHEST
    raw_part = jnp.einsum(
        "tic,kic->tk", streams, merge_rows, precision=highest, preferred_element_type=jnp.float32
    )
    gram_part = jnp.einsum("tic,tjc->tij", streams, streams, preferred_element_type=jnp.float32)
    columns = jnp.concatenate([raw_part, jnp.trace(gram_part, axis1=1, axis2=2)[:, None]], axis=1)

    def finish_first(summed):
        post_mix, residual_blend = first_coef(
            summed[:, :20], summed[:, 20], blend_bias, blend_scale
        )
        return jnp.concatenate([post_mix, residual_blend.reshape(-1, 16)], axis=1)

    merge_coef = settle(columns, finish_first)
    post_mix = merge_coef[:, :4]
    residual_blend = merge_coef[:, 4:20].reshape(-1, 4, 4)
    mixed = mix_streams(residual_blend, post_mix, streams, branch_out)
    streams_out = mixed.astype(jnp.bfloat16)
    raw_next = jnp.einsum("tic,kic->tk", mixed, next_rows, precision=highest)
    extra_cols = jnp.sum(mixed * mixed, axis=(1, 2))[:, None]
    columns_next = jnp.concatenate([raw_next, extra_cols], axis=1)

    def finish_second(summed):
        squares = summed[:, 24]
        pre_next, post_next, residual_following = second_coef(
            summed[:, :24], squares, blend_bias, blend_scale
        )
        pieces = [pre_next, post_next, residual_following.reshape(-1, 16)]
        return jnp.concatenate(pieces, axis=1)

    next_coef = settle(columns_next, finish_second)
    pre_next = next_coef[:, :4]
    next_mix = next_coef[:, 4:24]
    united = unite(pre_next, mixed)
    united_sq = lax.psum(jnp.sum(united * united, axis=1), "mp")
    branch_in = (united / jnp.sqrt(united_sq / D + epsilon)[:, None] * norm_gain).astype(
        jnp.bfloat16
    )
    return (streams_out, branch_in, next_mix)


def solution(mesh):
    placed = (
        P("dp", None, "mp"),
        P("dp", "mp"),
        P(None, None, ("mp", "dp")),
        P(None, None, ("mp", "dp")),
        P(),
        P(),
        P("mp"),
    )
    return jax.shard_map(
        local,
        mesh=mesh,
        in_specs=placed,
        out_specs=(P("dp", None, "mp"), P("dp", "mp"), P("dp", None)),
        check_vma=False,
    )
```

profile of v0, /device:TPU:0, one launch (start us, length us, event | category | flops | bytes accessed | tf_op | source)
XLA Modules:
  0.0 152.0 jit_solution(15976659351027897930)
XLA Ops:
  0.6 0.0 copy-start.7
  0.7 0.0 copy-start.8
  0.7 0.0 copy-start.6
  0.7 0.0 copy-start.5
  0.7 9.4 %fusion.28 = f32[256]{0:T(256)S(1)} fusion(bf16[256,4,2048]{2,1,0:T(4,128)(2,1)} %param.7, pred[4,4]{1,0:T(4,128)(4,1)S(1)} %iota_compare_fusion), kind=kOutput, calls=%fused_computation.54 | convolution fusion | flops 16785152 | bytes 4195344 | tf_op jit(solution)/shard_map/tic,tjc->tij/dot_general | solution.py:81
  10.1 0.0 copy-done.7
  10.1 0.1 fusion.80
  10.2 0.1 add.136
  10.2 0.1 fusion.79
  10.3 0.1 add.168
  10.4 0.0 copy-done.8
  10.4 0.6 fusion.78
  11.0 0.0 copy-done.6
  11.0 0.0 copy-done.5
  11.1 33.9 %all_gather.7 = f32[24,4,2048]{2,0,1:T(8,128)S(1)} all-gather(f32[24,4,256]{2,0,1:T(8,128)S(1)} %copy.16), channel_id=1, replica_groups=mesh['dp'=8,'mp'=4] {'dp'}, dimensions={2}, use_global_device_ids=true | all-gather | bytes 884736 | tf_op jit(solution)/shard_map/all_gather | solution.py:75
  45.0 32.1 %all_gather.6 = f32[20,4,2048]{2,0,1:T(8,128)S(1)} all-gather(f32[20,4,256]{2,0,1:T(8,128)S(1)} %copy.10), channel_id=1, replica_groups=mesh['dp'=8,'mp'=4] {'dp'}, dimensions={2}, use_global_device_ids=true | all-gather | bytes 737280 | tf_op jit(solution)/shard_map/all_gather | solution.py:74
  77.1 9.2 %convolution_bitcast_fusion = f32[256,20]{0,1:T(8,128)S(1)} fusion(f32[20,4,2048]{2,0,1:T(8,128)S(1)} %all_gather.6, bf16[256,4,2048]{2,1,0:T(4,128)(2,1)} %param.7), kind=kOutput, calls=%fused_computation.56 | convolution fusion | flops 503316480 | bytes 4870144 | tf_op jit(solution)/shard_map/tic,kic->tk/dot_general | solution.py:78
  86.3 10.4 %psum.21 = f32[256,21]{0,1:T(8,128)S(1)} all-reduce(f32[256,21]{0,1:T(8,128)S(1)} %pad_maximum_fusion.5), channel_id=1, replica_groups=mesh['dp'=8,'mp'=4] {'mp'}, use_global_device_ids=true, to_apply=%region_1.2 | all-reduce | flops 5376 | bytes 43008 | tf_op jit(solution)/shard_map/psum | solution.py:20
  96.7 0.8 fusion.56
  97.5 0.7 slice_multiply_fusion.1
  98.2 0.1 fusion.74
  98.6 0.0 copy-start.4
  98.6 4.6 %copy.11 = bf16[256,4,2048]{2,0,1:T(8,128)(2,1)S(1)} copy(bf16[256,4,2048]{2,1,0:T(4,128)(2,1)} %param.7) | data formatting | bytes 8388608 | tf_op args[0]
  103.2 0.0 copy-done.4
  103.2 2.3 %fusion.13 = (f32[256,2048]{1,0:T(8,128)S(1)}, f32[256,2048]{1,0:T(8,128)S(1)}) fusion(bf16[256,2048]{1,0:T(8,128)(2,1)S(1)} %copy-done.4, f32[256]{0:T(256)S(1)} %bitcast.135, f32[256]{0:T(256)S(1)} %bitcast.136, f32[256]{0:T(256)S(1)} %bitcast.137, f32[256]{0:T(256)S(1)} %bitcast.130, f32[256]{0:T(256)S(1)} %bitcast.140, ...), kind=kLoop, calls=%fused_computation.35 | loop fusion | flops 12058624 | bytes 9447424 | tf_op jit(solution)/shard_map/add | solution.py:58
  105.5 0.0 copy-start
  105.5 2.3 %fusion.21 = (f32[256,2048]{1,0:T(8,128)S(1)}, f32[256,2048]{1,0:T(8,128)S(1)}) fusion(bf16[256,2048]{1,0:T(8,128)(2,1)S(1)} %copy-done.4, f32[256]{0:T(256)S(1)} %bitcast.126, f32[256]{0:T(256)S(1)} %bitcast.127, f32[256]{0:T(256)S(1)} %bitcast.128, f32[256]{0:T(256)S(1)} %bitcast.129, f32[256]{0:T(256)S(1)} %bitcast.139, ...), kind=kLoop, calls=%fused_computation.43 | loop fusion | flops 12058624 | bytes 9447424 | tf_op jit(solution)/shard_map/add | solution.py:58
  107.8 0.0 copy-start.2
  107.8 0.0 copy-start.3
  107.8 6.6 %fusion.29 = f32[256,24]{0,1:T(8,128)S(1)} fusion(f32[24,4,2048]{2,0,1:T(8,128)S(1)} %all_gather.7, f32[256,1,2048]{2,0,1:T(8,128)S(1)} %bitcast.111, f32[256,1,2048]{2,0,1:T(8,128)S(1)} %bitcast.108, f32[256,1,2048]{2,0,1:T(8,128)S(1)} %bitcast.105, f32[256,1,2048]{2,0,1:T(8,128)S(1)} %bitcast.102), kind=kOutput, calls=%fused_computation.55 | convolution fusion | flops 610271232 | bytes 9199616 | tf_op jit(solution)/shard_map/tic,kic->tk/dot_general | solution.py:95
  114.4 0.0 copy-done
  114.4 0.0 copy-done.2
  114.4 0.0 copy-done.3
  114.4 0.9 multiply_reduce_fusion
  115.3 10.8 %psum.22 = f32[256,25]{0,1:T(8,128)S(1)} all-reduce(f32[256,25]{0,1:T(8,128)S(1)} %pad_maximum_fusion.4), channel_id=1, replica_groups=mesh['dp'=8,'mp'=4] {'mp'}, use_global_device_ids=true, to_apply=%region_15.16 | all-reduce | flops 6400 | bytes 51200 | tf_op jit(solution)/shard_map/psum | solution.py:20
  126.1 1.4 fusion.45
  127.5 0.6 slice_multiply_fusion
  128.1 0.1 fusion.72
  128.2 0.1 divide_reduce_fusion
  128.3 0.1 divide_reduce_fusion.6
  128.4 0.1 divide_reduce_fusion.5
  128.5 0.1 divide_reduce_fusion.4
  128.7 0.1 divide_reduce_fusion.3
  128.8 0.1 divide_reduce_fusion.2
  128.9 0.7 exponential_divide_fusion
  129.6 0.6 pad_maximum_fusion.6
  130.2 0.0 copy-start.9
  130.2 4.9 %multiply_reduce_fusion.1 = (f32[256]{0:T(256)S(1)}, f32[256,2048]{1,0:T(8,128)}) fusion(f32[256,2048]{1,0:T(8,128)} %copy-done.3, f32[256]{0:T(256)S(1)} %bitcast.143, f32[256,2048]{1,0:T(8,128)} %copy-done.2, f32[256]{0:T(256)S(1)} %bitcast.144, f32[256,2048]{1,0:T(8,128)} %copy-done, f32[256]{0:T(256)S(1)} %bitcast.145, ...), kind=kLoop, calls=%fused_computation.49 | loop fusion | flops 4718336 | bytes 10490880 | tf_op jit(solution)/shard_map/reduce_sum | solution.py:111
  135.1 5.9 %psum.23 = f32[256]{0:T(256)S(1)} all-reduce(f32[256]{0:T(256)S(1)} %get-tuple-element.6), channel_id=1, replica_groups=mesh['dp'=8,'mp'=4] {'mp'}, use_global_device_ids=true, to_apply=%region_17.18 | all-reduce | flops 256 | bytes 2048 | tf_op jit(solution)/shard_map/psum | solution.py:111
  141.0 0.0 copy-start.1
  141.0 0.0 copy-done.9
  141.1 3.0 %multiply_convert_fusion = bf16[256,2048]{1,0:T(8,128)(2,1)} fusion(f32[256,2048]{1,0:T(8,128)} %get-tuple-element.7, f32[2048]{0:T(1024)S(1)} %copy-done.9, f32[256]{0:T(256)S(1)} %add_sqrt_fusion), kind=kLoop, calls=%fused_computation.48 | loop fusion | flops 1572864 | bytes 3154944 | tf_op jit(solution)/shard_map/convert_element_type | solution.py:112
  144.1 0.0 copy-done.1
  144.1 2.6 %fusion.27 = bf16[256,4,2048]{2,0,1:T(8,128)(2,1)S(1)} fusion(f32[256,1,2048]{2,0,1:T(8,128)} %bitcast.113, f32[256,1,2048]{2,0,1:T(8,128)} %bitcast.110, f32[256,1,2048]{2,0,1:T(8,128)S(1)} %bitcast.107, f32[256,1,2048]{2,0,1:T(8,128)S(1)} %bitcast.104), kind=kLoop, calls=%fused_computation.52 | loop fusion | flops 6291456 | bytes 12582912 | tf_op jit(solution)/shard_map/convert_element_type | solution.py:94
  146.7 5.3 %copy.17 = bf16[256,4,2048]{2,1,0:T(4,128)(2,1)} copy(bf16[256,4,2048]{2,0,1:T(8,128)(2,1)S(1)} %fusion.27) | data formatting | bytes 8388608
  (26 shorter events, 0.4 us)
Async XLA Ops:
  0.6 9.4 %copy-start.7 = (f32[44]{0:T(128)S(1)}, f32[44]{0:T(128)}, u32[]{:S(2)}) copy-start(f32[44]{0:T(128)} %param.11) | copy-start | bytes 532
  0.7 9.8 %copy-start.8 = (f32[5]{0:T(128)S(1)}, f32[5]{0:T(128)}, u32[]{:S(2)}) copy-start(f32[5]{0:T(128)} %param.12) | copy-start | bytes 64
  0.7 10.4 %copy-start.6 = (f32[20,4,256]{2,1,0:T(4,128)S(1)}, f32[20,4,256]{2,1,0:T(4,128)}, u32[]{:S(2)}) copy-start(f32[20,4,256]{2,1,0:T(4,128)} %param.9) | copy-start | bytes 245764
  0.7 10.4 %copy-start.5 = (f32[24,4,256]{2,1,0:T(4,128)S(1)}, f32[24,4,256]{2,1,0:T(4,128)}, u32[]{:S(2)}) copy-start(f32[24,4,256]{2,1,0:T(4,128)} %param.10) | copy-start | bytes 294916
  98.6 4.6 %copy-start.4 = (bf16[256,2048]{1,0:T(8,128)(2,1)S(1)}, bf16[256,2048]{1,0:T(8,128)(2,1)}, u32[]{:S(2)}) copy-start(bf16[256,2048]{1,0:T(8,128)(2,1)} %param.8) | copy-start | bytes 3145732
  105.5 8.9 %copy-start = (f32[256,2048]{1,0:T(8,128)}, f32[256,2048]{1,0:T(8,128)S(1)}, u32[]{:S(2)}) copy-start(f32[256,2048]{1,0:T(8,128)S(1)} %get-tuple-element.11) | copy-start | bytes 6291460
  107.8 6.6 %copy-start.2 = (f32[256,2048]{1,0:T(8,128)}, f32[256,2048]{1,0:T(8,128)S(1)}, u32[]{:S(2)}) copy-start(f32[256,2048]{1,0:T(8,128)S(1)} %get-tuple-element.12) | copy-start | bytes 6291460
  107.8 6.6 %copy-start.3 = (f32[256,2048]{1,0:T(8,128)}, f32[256,2048]{1,0:T(8,128)S(1)}, u32[]{:S(2)}) copy-start(f32[256,2048]{1,0:T(8,128)S(1)} %get-tuple-element.13) | copy-start | bytes 6291460
  130.2 10.8 %copy-start.9 = (f32[2048]{0:T(1024)S(1)}, f32[2048]{0:T(1024)}, u32[]{:S(2)}) copy-start(f32[2048]{0:T(1024)} %param.13) | copy-start | bytes 24580
  141.0 3.1 %copy-start.1 = (f32[256,2048]{1,0:T(8,128)S(1)}, f32[256,2048]{1,0:T(8,128)}, u32[]{:S(2)}) copy-start(f32[256,2048]{1,0:T(8,128)} %copy-done) | copy-start | bytes 6291460
where the time goes:
time: 152 us
  blocking collectives  93.1 us (61%)
  matrix products  25.2 us (17%)
  other arithmetic  21.8 us (14%)
  local copies, waits for them, and re-layouts  10.9 us (7%)
    all_gather x1, blocking collectives, local(): lax.all_gather(next_weight, 'dp', axis=2, tiled=True)  33.9 us
    all_gather x1, blocking collectives, local(): lax.all_gather(merge_weight, 'dp', axis=2, tiled=True)  32.1 us
    psum x2, blocking collectives, settle(): summed = lax.psum(columns, 'mp')  21.2 us
    unnamed x26, local copies, waits for them, and re-layouts  9.92 us
    dot_general x1, matrix products, local(): jnp.einsum('tic,tjc->tij', streams, streams, preferred_element_type=jnp.f...  9.4 us
    dot_general x1, matrix products, local(): jnp.einsum('tic,kic->tk', streams, merge_rows, precision=highest, preferr...  9.18 us
    dot_general x1, matrix products, local(): raw_next = jnp.einsum('tic,kic->tk', mixed, next_rows, precision=highest)  6.59 us
    psum x1, blocking collectives, local(): united_sq = lax.psum(jnp.sum(united * united, axis=1), 'mp')  5.92 us

commit v1 on v0

--- a/solution.py
+++ b/solution.py
@@ -17,7 +17,9 @@
 
 
 def settle(columns, finish):
-    summed = lax.psum(columns, "mp")
+    summed = columns
+    for hop in (1, 2):
+        summed = summed + lax.ppermute(summed, "mp", [(dev, dev ^ hop) for dev in range(4)])
     result = finish(summed)
     return result
 

time: 152 us -> 139 us (0.914)
  blocking collectives: 93.1 us -> 74.8 us
  other arithmetic: 21.8 us -> 24.3 us
  starting transfers between devices: 0 us -> 2.23 us
  matrix products: 25.2 us -> 23.1 us
  local copies, waits for them, and re-layouts: 10.9 us -> 12.6 us
    psum x2 -> x0, blocking collectives: 21.2 us -> none  [settle(): summed = lax.psum(columns, 'mp')]
    ppermute x0 -> x4, starting transfers between devices: none -> 2.23 us  [settle(): lax.ppermute(summed, 'mp', [(dev, dev ^ hop) for dev in range(4)])]
    dot_general x1, matrix products: 9.18 us -> 6.99 us  [local(): jnp.einsum('tic,kic->tk', streams, merge_rows, precision=highest, preferr...]
    all_gather x1, blocking collectives: 32.1 us -> 33.9 us  [local(): lax.all_gather(merge_weight, 'dp', axis=2, tiled=True)]
    add x2, other arithmetic: 4.55 us -> 6.26 us  [mix_streams(): total + residual_blend[:, target, source, None] * streams[:, source, :].a...]
    unnamed x26 -> x28, local copies, waits for them, and re-layouts: 9.92 us -> 11.6 us
  transfers between devices with their start and end apart: 0 -> 4, of which waited for: 0 -> 1; matrix products, arithmetic and copies ran while one was open for 0% -> 10% of each run, Pallas kernels for 0% -> 0%
where the time goes in v1:
time: 139 us
  blocking collectives  74.8 us (54%)
  other arithmetic  24.3 us (17%)
  matrix products  23.1 us (17%)
  local copies, waits for them, and re-layouts  12.6 us (9%)
  starting transfers between devices  2.23 us (2%)
    all_gather x1, blocking collectives, local(): lax.all_gather(next_weight, 'dp', axis=2, tiled=True)  34 us
    all_gather x1, blocking collectives, local(): lax.all_gather(merge_weight, 'dp', axis=2, tiled=True)  33.9 us
    unnamed x28, local copies, waits for them, and re-layouts  11.6 us
    dot_general x1, matrix products, local(): jnp.einsum('tic,tjc->tij', streams, streams, preferred_element_type=jnp.f...  9.5 us
    dot_general x1, matrix products, local(): jnp.einsum('tic,kic->tk', streams, merge_rows, precision=highest, preferr...  6.99 us
    psum x1, blocking collectives, local(): united_sq = lax.psum(jnp.sum(united * united, axis=1), 'mp')  6.83 us
    dot_general x1, matrix products, local(): raw_next = jnp.einsum('tic,kic->tk', mixed, next_rows, precision=highest)  6.59 us
    add x2, other arithmetic, mix_streams(): total + residual_blend[:, target, source, None] * streams[:, source, :].a...  6.26 us
  transfers between devices with their start and end apart: 4, of which 1 were waited for; matrix products, arithmetic and copies ran while one was open for 10% of the time, Pallas kernels for 0%

profile of v1, /device:TPU:0, one launch (start us, length us, event | category | flops | bytes accessed | tf_op | source)
XLA Modules:
  0.0 139.1 jit_solution(13697419002741713066)
XLA Ops:
  0.6 0.9 copy.10
  1.6 33.9 %all_gather.6 = f32[20,4,2048]{2,0,1:T(8,128)S(1)} all-gather(f32[20,4,256]{2,0,1:T(8,128)S(1)} %copy.10), channel_id=1, replica_groups=mesh['dp'=8,'mp'=4] {'dp'}, dimensions={2}, use_global_device_ids=true | all-gather | bytes 737280 | tf_op jit(solution)/shard_map/all_gather | solution.py:76
  35.4 0.0 copy-start.4
  35.4 9.5 %fusion.28 = f32[256]{0:T(256)S(1)} fusion(bf16[256,4,2048]{2,1,0:T(4,128)(2,1)} %param.7, pred[4,4]{1,0:T(4,128)(4,1)S(1)} %iota_compare_fusion), kind=kOutput, calls=%fused_computation.54 | convolution fusion | flops 16785152 | bytes 4195344 | tf_op jit(solution)/shard_map/tic,tjc->tij/dot_general | solution.py:83
  44.9 0.0 copy-done.4
  44.9 0.0 copy-start.8
  44.9 0.0 copy-start.7
  45.0 0.0 copy-start.9
  45.0 7.0 %convolution_bitcast_fusion = f32[256,20]{0,1:T(8,128)S(1)} fusion(f32[20,4,2048]{2,0,1:T(8,128)S(1)} %all_gather.6, bf16[256,4,2048]{2,1,0:T(4,128)(2,1)S(1)} %copy-done.4), kind=kOutput, calls=%fused_computation.56 | convolution fusion | flops 503316480 | bytes 4870144 | tf_op jit(solution)/shard_map/tic,kic->tk/dot_general | solution.py:80
  52.0 0.1 collective-permute-start
  52.1 0.0 copy-done.8
  52.1 0.1 fusion.80
  52.1 0.0 copy-done.7
  52.2 34.0 %all_gather.7 = f32[24,4,2048]{2,0,1:T(8,128)} all-gather(f32[24,4,256]{2,0,1:T(8,128)S(1)} %copy.16), channel_id=1, replica_groups=mesh['dp'=8,'mp'=4] {'dp'}, dimensions={2}, use_global_device_ids=true | all-gather | bytes 884736 | tf_op jit(solution)/shard_map/all_gather | solution.py:77
  86.2 0.1 fusion.81
  86.3 0.0 collective-permute-done
  86.3 1.6 %collective-permute-start.1 = (f32[256,21]{0,1:T(8,128)S(1)}, f32[256,21]{0,1:T(8,128)S(1)}, u32[]{:S(2)}, u32[]{:S(2)}) collective-permute-start(f32[256,21]{0,1:T(8,128)S(1)} %fusion.86), channel_id=1, source_target_pairs={{0,2},{1,3},{2,0},{3,1},{4,6},{5,7},{6,4},{7,5},{8,10},{9,11},{10,... | collective-permute-start | bytes 64520 | tf_op jit(solution)/shard_map/ppermute | solution.py:22
  87.9 0.0 copy-done.9
  87.9 0.7 fusion.79
  88.5 4.3 %copy.11 = bf16[256,4,2048]{2,0,1:T(8,128)(2,1)} copy(bf16[256,4,2048]{2,1,0:T(4,128)(2,1)S(1)} %copy-done.4) | data formatting | bytes 8388608 | tf_op args[0]
  92.8 0.0 copy-start.5
  92.8 0.1 add.146
  92.9 0.0 collective-permute-done.1
  93.0 0.8 slice_multiply_fusion.1
  93.7 0.6 fusion.56
  94.4 0.1 fusion.75
  94.8 0.0 copy-done.5
  94.8 0.0 copy-start
  94.8 4.0 %fusion.13 = (f32[256,2048]{1,0:T(8,128)S(1)}, f32[256,2048]{1,0:T(8,128)S(1)}) fusion(bf16[256,2048]{1,0:T(8,128)(2,1)S(1)} %copy-done.5, f32[256]{0:T(256)S(1)} %bitcast.138, f32[256]{0:T(256)S(1)} %bitcast.139, f32[256]{0:T(256)S(1)} %bitcast.140, f32[256]{0:T(256)S(1)} %bitcast.133, f32[256]{0:T(256)S(1)} %bitcast.143, bf16[256,4,2048]{2,0,1:T(8,128)(2,1)} %copy.11, ...), kind=kLoop, calls=%fused_computation.35 | loop fusion | flops 12058624 | bytes 9447424 | tf_op jit(solution)/shard_map/add | solution.py:60
  98.8 0.0 copy-start.1
  98.8 0.0 copy-done
  98.8 2.3 %fusion.21 = (f32[256,2048]{1,0:T(8,128)S(1)}, f32[256,2048]{1,0:T(8,128)S(1)}) fusion(bf16[256,2048]{1,0:T(8,128)(2,1)S(1)} %copy-done.5, f32[256]{0:T(256)S(1)} %bitcast.127, f32[256]{0:T(256)S(1)} %bitcast.128, f32[256]{0:T(256)S(1)} %bitcast.129, f32[256]{0:T(256)S(1)} %bitcast.130, f32[256]{0:T(256)S(1)} %bitcast.142, ...), kind=kLoop, calls=%fused_computation.43 | loop fusion | flops 12058624 | bytes 9447424 | tf_op jit(solution)/shard_map/add | solution.py:60
  101.1 0.0 copy-start.2
  101.1 0.0 copy-start.3
  101.1 0.0 copy-start.6
  101.1 0.9 multiply_reduce_fusion
  102.0 0.0 copy-done.1
  102.0 0.4 copy-done.2
  102.4 0.7 copy-done.3
  103.1 0.0 copy-done.6
  103.1 6.6 %fusion.29 = f32[256,24]{0,1:T(8,128)S(1)} fusion(f32[24,4,2048]{2,0,1:T(8,128)S(1)} %copy-done.6, f32[256,1,2048]{2,0,1:T(8,128)S(1)} %bitcast.112, f32[256,1,2048]{2,0,1:T(8,128)S(1)} %bitcast.109, f32[256,1,2048]{2,0,1:T(8,128)S(1)} %bitcast.106, f32[256,1,2048]{2,0,1:T(8,128)S(1)} %bitcast.103), kind=kOutput, calls=%fused_computation.55 | convolution fusion | flops 610271232 | bytes 9199616 | tf_op jit(solution)/shard_map/tic,kic->tk/dot_general | solution.py:97
  109.7 0.1 collective-permute-start.2
  109.8 0.1 add.180
  109.9 1.1 collective-permute-done.2
  111.0 0.5 collective-permute-start.3
  111.5 3.5 %fusion.27 = bf16[256,4,2048]{2,0,1:T(8,128)(2,1)S(1)} fusion(f32[256,1,2048]{2,0,1:T(8,128)} %bitcast.113, f32[256,1,2048]{2,0,1:T(8,128)} %bitcast.110, f32[256,1,2048]{2,0,1:T(8,128)} %bitcast.107, f32[256,1,2048]{2,0,1:T(8,128)S(1)} %bitcast.104), kind=kLoop, calls=%fused_computation.52 | loop fusion | flops 6291456 | bytes 12582912 | tf_op jit(solution)/shard_map/convert_element_type | solution.py:96
  115.0 5.3 %copy.17 = bf16[256,4,2048]{2,1,0:T(4,128)(2,1)} copy(bf16[256,4,2048]{2,0,1:T(8,128)(2,1)S(1)} %fusion.27) | data formatting | bytes 8388608
  120.2 0.0 collective-permute-done.3
  120.3 1.4 fusion.45
  121.7 0.6 slice_multiply_fusion
  122.3 0.1 fusion.73
  122.4 0.1 divide_reduce_fusion
  122.5 0.1 divide_reduce_fusion.6
  122.6 0.1 divide_reduce_fusion.5
  122.7 0.1 divide_reduce_fusion.4
  122.8 0.1 divide_reduce_fusion.3
  123.0 0.1 divide_reduce_fusion.2
  123.1 0.7 exponential_divide_fusion
  123.8 0.0 copy-start.10
  123.8 4.9 %multiply_reduce_fusion.1 = (f32[256]{0:T(256)S(1)}, f32[256,2048]{1,0:T(8,128)}) fusion(f32[256,2048]{1,0:T(8,128)} %copy-done.3, f32[256]{0:T(256)S(1)} %bitcast.146, f32[256,2048]{1,0:T(8,128)} %copy-done.2, f32[256]{0:T(256)S(1)} %bitcast.147, f32[256,2048]{1,0:T(8,128)} %copy-done.1, f32[256]{0:T(256)S(1)} %bitcast.148, ...), kind=kLoop, calls=%fused_computation.49 | loop fusion | flops 4718336 | bytes 10490880 | tf_op jit(solution)/shard_map/reduce_sum | solution.py:113
  128.7 6.8 %psum.7 = f32[256]{0:T(256)S(1)} all-reduce(f32[256]{0:T(256)S(1)} %get-tuple-element.6), channel_id=1, replica_groups=mesh['dp'=8,'mp'=4] {'mp'}, use_global_device_ids=true, to_apply=%region_15.16 | all-reduce | flops 256 | bytes 2048 | tf_op jit(solution)/shard_map/psum | solution.py:113
  135.6 0.6 pad_maximum_fusion.6
  136.2 0.0 copy-done.10
  136.2 2.9 %multiply_convert_fusion = bf16[256,2048]{1,0:T(8,128)(2,1)} fusion(f32[256,2048]{1,0:T(8,128)} %get-tuple-element.7, f32[2048]{0:T(1024)S(1)} %copy-done.10, f32[256]{0:T(256)S(1)} %add_sqrt_fusion), kind=kLoop, calls=%fused_computation.48 | loop fusion | flops 1572864 | bytes 3154944 | tf_op jit(solution)/shard_map/convert_element_type | solution.py:114
  (29 shorter events, 0.4 us)
Async XLA Ops:
  35.4 9.5 %copy-start.4 = (bf16[256,4,2048]{2,1,0:T(4,128)(2,1)S(1)}, bf16[256,4,2048]{2,1,0:T(4,128)(2,1)}, u32[]{:S(2)}) copy-start(bf16[256,4,2048]{2,1,0:T(4,128)(2,1)} %param.7) | copy-start | bytes 12582916
  44.9 7.1 %copy-start.8 = (f32[44]{0:T(128)S(1)}, f32[44]{0:T(128)}, u32[]{:S(2)}) copy-start(f32[44]{0:T(128)} %param.11) | copy-start | bytes 532
  44.9 7.2 %copy-start.7 = (f32[24,4,256]{2,1,0:T(4,128)S(1)}, f32[24,4,256]{2,1,0:T(4,128)}, u32[]{:S(2)}) copy-start(f32[24,4,256]{2,1,0:T(4,128)} %param.10) | copy-start | bytes 294916
  45.0 42.9 %copy-start.9 = (f32[5]{0:T(128)S(1)}, f32[5]{0:T(128)}, u32[]{:S(2)}) copy-start(f32[5]{0:T(128)} %param.12) | copy-start | bytes 64
  52.0 34.3 %collective-permute-start = (f32[256,21]{0,1:T(8,128)S(1)}, f32[256,21]{0,1:T(8,128)S(1)}, u32[]{:S(2)}, u32[]{:S(2)}) collective-permute-start(f32[256,21]{0,1:T(8,128)S(1)} %pad_maximum_fusion.5), channel_id=1, source_target_pairs={{0,1},{1,0},{2,3},{3,2},{4,5},{5,4},{6,7},{7,6},{8,9},{9,8},{10,11... | collective-permute-start | bytes 64520 | tf_op jit(solution)/shard_map/ppermute | solution.py:22
  86.3 6.6 %collective-permute-start.1 = (f32[256,21]{0,1:T(8,128)S(1)}, f32[256,21]{0,1:T(8,128)S(1)}, u32[]{:S(2)}, u32[]{:S(2)}) collective-permute-start(f32[256,21]{0,1:T(8,128)S(1)} %fusion.86), channel_id=1, source_target_pairs={{0,2},{1,3},{2,0},{3,1},{4,6},{5,7},{6,4},{7,5},{8,10},{9,11},{10,... | collective-permute-start | bytes 64520 | tf_op jit(solution)/shard_map/ppermute | solution.py:22
  92.8 1.9 %copy-start.5 = (bf16[256,2048]{1,0:T(8,128)(2,1)S(1)}, bf16[256,2048]{1,0:T(8,128)(2,1)}, u32[]{:S(2)}) copy-start(bf16[256,2048]{1,0:T(8,128)(2,1)} %param.8) | copy-start | bytes 3145732
  94.8 4.0 %copy-start = (bf16[256,4,2048]{2,0,1:T(8,128)(2,1)S(1)}, bf16[256,4,2048]{2,0,1:T(8,128)(2,1)}, u32[]{:S(2)}) copy-start(bf16[256,4,2048]{2,0,1:T(8,128)(2,1)} %copy.11) | copy-start | bytes 12582916
  98.8 3.2 %copy-start.1 = (f32[256,2048]{1,0:T(8,128)}, f32[256,2048]{1,0:T(8,128)S(1)}, u32[]{:S(2)}) copy-start(f32[256,2048]{1,0:T(8,128)S(1)} %get-tuple-element.11) | copy-start | bytes 6291460
  101.1 1.3 copy-start.2
  101.1 2.0 %copy-start.3 = (f32[256,2048]{1,0:T(8,128)}, f32[256,2048]{1,0:T(8,128)S(1)}, u32[]{:S(2)}) copy-start(f32[256,2048]{1,0:T(8,128)S(1)} %get-tuple-element.13) | copy-start | bytes 6291460
  101.1 2.0 %copy-start.6 = (f32[24,4,2048]{2,0,1:T(8,128)S(1)}, f32[24,4,2048]{2,0,1:T(8,128)}, u32[]{:S(2)}) copy-start(f32[24,4,2048]{2,0,1:T(8,128)} %all_gather.7) | copy-start | bytes 2359300
  109.7 1.3 collective-permute-start.2
  111.0 9.3 %collective-permute-start.3 = (f32[256,25]{0,1:T(8,128)S(1)}, f32[256,25]{0,1:T(8,128)S(1)}, u32[]{:S(2)}, u32[]{:S(2)}) collective-permute-start(f32[256,25]{0,1:T(8,128)S(1)} %fusion.62), channel_id=1, source_target_pairs={{0,2},{1,3},{2,0},{3,1},{4,6},{5,7},{6,4},{7,5},{8,10},{9,11},{10,... | collective-permute-start | bytes 76808 | tf_op jit(solution)/shard_map/ppermute | solution.py:22
  123.8 12.4 %copy-start.10 = (f32[2048]{0:T(1024)S(1)}, f32[2048]{0:T(1024)}, u32[]{:S(2)}) copy-start(f32[2048]{0:T(1024)} %param.13) | copy-start | bytes 24580
